TPU v7x, 256 devices: a whole 4x4x8 slice. The times are simulated.
256 devices in a mesh: tm: 8 (over x, core), space: 32 (over z, y).
Axes of the slice: x: 4, y: 4, z: 8, core: 2. Of those that a mesh axis runs over, the one named last changes fastest.
Arguments:
- video_in: bfloat16 [32, 32, 16, 3072], P('tm', 'space'), may hold values from -6 to 6
- neighbours: int32 [32, 8], replicated, may hold values from 0 to 32, as said below
- valid_frames: int32 [32], replicated, may hold values from 0 to 32, as said below
- norm1_gain: float32 [192], replicated, may hold values from 0.1 to 1.9
- conv1_weight: bfloat16 [9, 576, 192], replicated, may hold values from -0.078125 to 0.078125
- conv1_bias: float32 [192], replicated, may hold values from -3 to 3
- norm2_gain: float32 [192], replicated, may hold values from 0.1 to 1.9
- conv2_weight: bfloat16 [9, 576, 192], replicated, may hold values from -0.078125 to 0.078125
- conv2_bias: float32 [192], replicated, may hold values from -3 to 3
Outputs:
- block_out: bfloat16 [32, 32, 16, 3072], P('tm', 'space')
Inputs may be any that keep to these rules, and one draw needn't show every extreme that they name: `neighbours`: entry k of a tile's row names the tile beside it in direction k of one placement of all tiles on a grid of 4 rows by 8 columns, directions ordered (row, column) = (-1,-1), (-1,0), (-1,1), (0,-1), (0,1), (1,-1), (1,0), (1,1); 32 where that place lies outside the grid. `valid_frames`: frames from this number on are padding in that tile's track.
All inputs are finite; a program needn't handle non-finite values.
Results may differ from a plain program's by a relative error of at most 0.0037.
Values may be sent and summed in bfloat16 or wider, within the bound.
A program may use at most 64 MiB of HBM per device.

v0:
```python
from functools import partial

import jax
import jax.numpy as jnp
from jax import lax
from jax.sharding import Mesh
from jax.sharding import PartitionSpec as P

SPACE = ("space_0", "space_1")


epsilon = 1e-06


def gather_axes(array, axes, dim):
    for axis in reversed(axes):
        array = lax.all_gather(array, axis, axis=dim, tiled=True)
    return array


def shifted(value, axis, steps):
    count = lax.axis_size(axis)
    first, last = (max(0, -steps), min(count, count - steps))
    return lax.ppermute(value, axis, [(source, source + steps) for source in range(first, last)])


def norm_silu(values, scale_gain):
    square = jnp.mean(values * values, axis=-1, keepdims=True)
    return jax.nn.silu(values * lax.rsqrt(square + epsilon) * scale_gain)


def conv_tile(framed, weight):
    frames_out = framed.shape[0] - 2
    side_len = framed.shape[1] - 2
    channels = framed.shape[-1]
    widened = jnp.concatenate(
        [framed[:, :, col_off : col_off + side_len] for col_off in range(3)], axis=-1
    )
    summed = jnp.zeros((frames_out * side_len * side_len, channels), jnp.float32)
    for time_off in range(3):
        for row_off in range(3):
            window = widened[
                time_off : time_off + frames_out, row_off : row_off + side_len
            ].reshape(-1, 3 * channels)
            summed = summed + jnp.dot(
                window, weight[time_off * 3 + row_off], preferred_element_type=jnp.float32
            )
    return summed.reshape(frames_out, side_len, side_len, channels)


def edge_pack(activation):
    return jnp.stack(
        [
            activation[:, :, -1],
            activation[:, :, :, -1],
            activation[:, :, :, 0],
            activation[:, :, 0],
        ],
        axis=2,
    )


def fold_edges(totals, portion, offset, nearby):
    amount = portion.shape[1]
    tile_ids = jnp.arange(amount, dtype=jnp.int32)
    choose = (nearby[:, :, None] == tile_ids[None, None, :]).astype(jnp.bfloat16)
    side_choose = jnp.stack([choose[:, 1], choose[:, 3], choose[:, 4], choose[:, 6]], axis=1)
    corner_choose = jnp.stack([choose[:, 0], choose[:, 2], choose[:, 5], choose[:, 7]], axis=1)
    corner_source = jnp.stack(
        [portion[:, :, 0, -1], portion[:, :, 0, 0], portion[:, :, 3, -1], portion[:, :, 3, 0]],
        axis=2,
    )
    new_sides = jnp.einsum(
        "djn,fnjxc->fdjxc", side_choose, portion, preferred_element_type=jnp.float32
    )
    new_corners = jnp.einsum(
        "djn,fnjc->fdjc", corner_choose, corner_source, preferred_element_type=jnp.float32
    )
    return (new_sides.astype(jnp.bfloat16), new_corners.astype(jnp.bfloat16))


def empty_rims(frame_count, activation):
    tiles_dev, side_len, channels = (activation.shape[1], activation.shape[2], activation.shape[4])
    return (
        jnp.zeros((frame_count, tiles_dev, 4, side_len, channels), jnp.bfloat16),
        jnp.zeros((frame_count, tiles_dev, 4, channels), jnp.bfloat16),
    )


def assemble(longer, side_rims, corners):
    top_row = jnp.concatenate([corners[:, :, 0:1], side_rims[:, :, 0], corners[:, :, 1:2]], axis=2)
    bottom_row = jnp.concatenate(
        [corners[:, :, 2:3], side_rims[:, :, 3], corners[:, :, 3:4]], axis=2
    )
    middle = jnp.concatenate(
        [side_rims[:, :, 1][:, :, :, None], longer, side_rims[:, :, 2][:, :, :, None]], axis=3
    )
    return jnp.concatenate([top_row[:, :, None], middle, bottom_row[:, :, None]], axis=2)


def extend(activation, nearby):
    frames_dev = activation.shape[0]
    folder = partial(fold_edges, nearby=nearby)
    side_rims, corners = folder(
        empty_rims(frames_dev, activation),
        gather_axes(edge_pack(activation), SPACE, 1),
        jnp.int32(0),
    )
    prev_act, prev_sides, prev_corners = shifted(
        (activation[frames_dev - 2 :], side_rims[frames_dev - 2 :], corners[frames_dev - 2 :]),
        "tm",
        1,
    )
    longer = jnp.concatenate([prev_act, activation], axis=0)
    side_rims = jnp.concatenate([prev_sides, side_rims], axis=0)
    corners = jnp.concatenate([prev_corners, corners], axis=0)
    return assemble(longer, side_rims, corners)


def blank_tile(pieces, tile_valid):
    framed = pieces[0]
    return jnp.zeros(
        (framed.shape[0] - 2, framed.shape[1] - 2, framed.shape[2] - 2, framed.shape[3]),
        jnp.bfloat16,
    )


def home_tiles(inputs, home_valid, first_frame, worker):
    pieces = tuple((stacked[:, 0] for stacked in inputs))
    results = [lax.cond(home_valid[0] > first_frame, worker, blank_tile, pieces, home_valid[0])]
    return jnp.stack(results, axis=1)


def on_device(
    video_in,
    neighbours,
    valid_frames,
    norm1_gain,
    conv1_weight,
    conv1_bias,
    norm2_gain,
    conv2_weight,
    conv2_bias,
):
    frames_dev, tiles_dev, side_len, merged = video_in.shape
    channels = norm1_gain.shape[0]
    voxels = video_in.reshape(frames_dev, tiles_dev, side_len, side_len, channels)
    first_frame = lax.axis_index("tm") * frames_dev
    home_ids = lax.axis_index(SPACE) * tiles_dev + jnp.arange(tiles_dev, dtype=jnp.int32)
    home_valid = jnp.take(valid_frames, home_ids)
    nearby = jnp.take(neighbours, home_ids, axis=0)
    frame_pos = first_frame + jnp.arange(frames_dev, dtype=jnp.int32)
    present = (frame_pos[:, None] < home_valid[None, :]).astype(jnp.bfloat16)
    masked = voxels * present[:, :, None, None, None]
    activation = norm_silu(masked.astype(jnp.float32), norm1_gain).astype(jnp.bfloat16)

    def frame_weights(tile_valid):
        return (frame_pos < tile_valid).astype(jnp.float32)[:, None, None, None]

    def first_worker(pieces, tile_valid):
        summed = conv_tile(pieces[0], conv1_weight)
        return norm_silu((summed + conv1_bias) * frame_weights(tile_valid), norm2_gain).astype(
            jnp.bfloat16
        )

    def second_worker(pieces, tile_valid):
        summed = conv_tile(pieces[0], conv2_weight)
        return (
            (summed + conv2_bias) * frame_weights(tile_valid) + pieces[1].astype(jnp.float32)
        ).astype(jnp.bfloat16)

    padded = extend(activation, nearby)
    hidden = home_tiles((padded,), home_valid, first_frame, first_worker)
    padded = extend(hidden, nearby)
    block_out = home_tiles((padded, masked), home_valid, first_frame, second_worker)
    return block_out.reshape(frames_dev, tiles_dev, side_len, side_len * channels)


def solution(mesh):
    split = Mesh(mesh.devices.reshape(mesh.shape["tm"], 8, 4), ("tm", "space_0", "space_1"))
    placed = (P("tm", SPACE, None, None), P(), P(), P(), P(), P(), P(), P(), P())
    return jax.shard_map(
        on_device,
        mesh=split,
        in_specs=placed,
        out_specs=P("tm", SPACE, None, None),
        check_vma=False,
    )
```

profile of v0, /device:TPU:2, one launch (start us, length us, event | category | flops | bytes accessed | tf_op | source)
XLA Modules:
  0.0 238.0 jit_solution(15837202351396522380)
XLA Ops:
  6.5 1.6 reshape.252
  8.2 1.3 dynamic-slice.5
  11.1 14.0 %all_gather.12 = bf16[4,4,4,16,192]{4,3,2,0,1:T(8,128)(2,1)} all-gather(bf16[4,1,4,16,192]{4,3,2,0,1:T(8,128)(2,1)S(1)} %pad_maximum_fusion.4), channel_id=1, replica_groups=mesh['tm'=8,'space_0'=8,'space_1'=4] {'space_1'}, dimensions={1}, use_global_device_ids=true | all-gather | bytes 491520 | tf_op jit(solution)/shard_map/all_gather | solution.py:17
  25.2 1.9 collective-permute-start.2
  27.5 55.5 %all-gather.3.cloned.1.call-done = bf16[4,32,4,16,192]{4,3,2,0,1:T(8,128)(2,1)} async-done(((bf16[4,4,4,16,192]{4,3,2,0,1:T(8,128)(2,1)}), bf16[4,32,4,16,192]{4,3,2,0,1:T(8,128)(2,1)}) %all-gather.3.cloned.1.call-update) | async-done | bytes 3145744 | tf_op jit(solution)/shard_map/all_gather | solution.py:17
  83.0 2.0 fusion.77
  85.3 1.9 collective-permute-start
  87.2 4.6 %fusion.4 = bf16[4,1,4,16,192]{4,1,3,2,0:T(2,128)(2,1)S(1)} fusion(bf16[4,32,4,16,192]{4,3,2,0,1:T(8,128)(2,1)} %all-gather.3.cloned.1.call-done, bf16[4,32,1,1,1]{1,0,2,3,4:T(4,128)(2,1)S(1)} %maximum_bitcast_fusion.3), kind=kOutput, calls=%fused_computation.47 | convolution fusion | flops 3145728 | bytes 3244288 | tf_op jit(solution)/shard_map/djn,fnjxc->fdjxc/dot_general | solution.py:73
  91.9 3.5 %collective-permute-start.1 = (bf16[2,1,4,16,192]{4,3,0,2,1:T(8,128)(2,1)S(1)}, bf16[2,1,4,16,192]{4,3,0,2,1:T(8,128)(2,1)S(1)}, u32[]{:S(2)}, u32[]{:S(2)}) collective-permute-start(bf16[2,1,4,16,192]{4,3,0,2,1:T(8,128)(2,1)S(1)} %slice.385), channel_id=1, source_target_pairs={{0,32},{32,64},{64,96},{96,128},{128,160},{160,192},{192,224},{1,3... | collective-permute-start | bytes 147464 | tf_op jit(solution)/shard_map/ppermute | solution.py:24
  95.4 2.0 collective-permute-done.1
  97.8 0.9 pad_maximum_fusion.2
  98.7 24.8 %conditional.2 = (bf16[4,16,16,192]{3,2,1,0:T(8,128)(2,1)S(1)}) conditional(s32[]{:T(128)} %convert_element_type.107, () %tuple.20, (bf16[6,1,18,18,192]{4,3,2,0,1:T(8,128)(2,1)S(1)}, bf16[9,576,192]{1,2,0:T(8,128)(2,1)}, f32[192]{0:T(256)S(1)}, s32[]{:T(128)}, s32[4]{0:T(128)S(1)}, /*index=5*/f32[192]{0:T(256)S(1)}) %tuple.106), branch_computations={%region_1.2_spmd, %region_2.4_spmd} | conditional | flops 2048533504 | bytes 96561936 | solution.py:130
  99.6 0.9 pad_maximum_fusion
  100.5 4.4 %fusion.72 = (bf16[4,16,16,576]{3,2,1,0:T(8,128)(2,1)}, bf16[4,16,16,576]{3,2,1,0:T(8,128)(2,1)}, bf16[4,16,16,576]{3,2,1,0:T(8,128)(2,1)}, bf16[4,16,16,576]{3,...) fusion(bf16[6,18,16,576]{3,2,1,0:T(8,128)(2,1)S(1)} %pad_maximu, ...), kind=kLoop, calls=%fused_computation.174 | loop fusion | bytes 21233664 | tf_op jit(solution)/shard_map/cond/branch_1_fun/slice | solution.py:42
  104.8 4.1 %copy.179 = bf16[9,576,192]{2,1,0:T(8,128)(2,1)S(1)} copy(bf16[9,576,192]{1,2,0:T(8,128)(2,1)} %get-tuple-element.168) | data formatting | bytes 3981312 | tf_op jit(solution)/shard_map
  108.9 2.0 fusion
  118.9 1.5 convolution_add_fusion.1
  120.5 2.2 multiply_reduce_fusion
  123.8 13.9 %all_gather.14 = bf16[4,4,4,16,192]{4,3,2,0,1:T(8,128)(2,1)} all-gather(bf16[4,1,4,16,192]{4,3,2,0,1:T(8,128)(2,1)S(1)} %pad_maximum_fusion.5), channel_id=1, replica_groups=mesh['tm'=8,'space_0'=8,'space_1'=4] {'space_1'}, dimensions={1}, use_global_device_ids=true | all-gather | bytes 491520 | tf_op jit(solution)/shard_map/all_gather | solution.py:17
  137.7 1.9 collective-permute-start.5
  139.6 51.6 %all-gather.5.cloned.1.call-done = bf16[4,32,4,16,192]{4,3,2,0,1:T(8,128)(2,1)} async-done(((bf16[4,4,4,16,192]{4,3,2,0,1:T(8,128)(2,1)}), bf16[4,32,4,16,192]{4,3,2,0,1:T(8,128)(2,1)}) %all-gather.5.cloned.1.call-update) | async-done | bytes 3145744 | tf_op jit(solution)/shard_map/all_gather | solution.py:17
  191.2 2.0 fusion.76
  193.5 1.9 collective-permute-start.3
  195.5 4.6 %fusion.2 = bf16[4,1,4,16,192]{4,1,3,2,0:T(2,128)(2,1)S(1)} fusion(bf16[4,32,4,16,192]{4,3,2,0,1:T(8,128)(2,1)} %all-gather.5.cloned.1.call-done, bf16[4,32,1,1,1]{1,0,2,3,4:T(4,128)(2,1)S(1)} %maximum_bitcast_fusion.3), kind=kOutput, calls=%fused_computation.45 | convolution fusion | flops 3145728 | bytes 3244288 | tf_op jit(solution)/shard_map/djn,fnjxc->fdjxc/dot_general | solution.py:73
  200.1 3.7 %collective-permute-start.4 = (bf16[2,1,4,16,192]{4,3,0,2,1:T(8,128)(2,1)S(1)}, bf16[2,1,4,16,192]{4,3,0,2,1:T(8,128)(2,1)S(1)}, u32[]{:S(2)}, u32[]{:S(2)}) collective-permute-start(bf16[2,1,4,16,192]{4,3,0,2,1:T(8,128)(2,1)S(1)} %slice.408), channel_id=1, source_target_pairs={{0,32},{32,64},{64,96},{96,128},{128,160},{160,192},{192,224},{1,3... | collective-permute-start | bytes 147464 | tf_op jit(solution)/shard_map/ppermute | solution.py:24
  203.9 1.8 collective-permute-done.4
  206.0 0.9 pad_maximum_fusion.3
  206.9 24.2 %conditional.3 = (bf16[4,1,16,3072]{3,2,0,1:T(8,128)(2,1)}) conditional(s32[]{:T(128)} %convert_element_type.107, () %tuple.19, (bf16[6,1,18,18,192]{4,3,2,0,1:T(8,128)(2,1)S(1)}, bf16[9,576,192]{1,2,0:T(8,128)(2,1)}, f32[192]{0:T(256)S(1)}, s32[]{:T(128)}, s32[4]{0:T(128)S(1)}, /*index=5*/bf16[4]{0:T(256)(128)(2,1)S(1)}, ...), branch_computations={%region_4.5_spmd, %region_5.6_spmd} | conditional | flops 2047156224 | bytes 104957008 | solution.py:130
  208.5 4.4 %fusion.74 = (bf16[4,16,16,576]{3,2,1,0:T(8,128)(2,1)}, bf16[4,16,16,576]{3,2,1,0:T(8,128)(2,1)}, bf16[4,16,16,576]{3,2,1,0:T(8,128)(2,1)}, bf16[4,16,16,576]{3,...) fusion(bf16[6,18,16,576]{3,2,1,0:T(8,128)(2,1)S(1)} %pad_maximu, ...), kind=kLoop, calls=%fused_computation.176 | loop fusion | bytes 21233664 | tf_op jit(solution)/shard_map/cond/branch_1_fun/slice | solution.py:42
  212.9 4.1 %copy.190 = bf16[9,576,192]{2,1,0:T(8,128)(2,1)S(1)} copy(bf16[9,576,192]{1,2,0:T(8,128)(2,1)} %get-tuple-element.174) | data formatting | bytes 3981312 | tf_op jit(solution)/shard_map
  217.0 2.0 fusion.1
  230.2 0.9 add_convert_fusion
  (131 shorter events, 24.8 us)
Async XLA Ops:
  6.5 3.9 %copy-start.18 = (f32[192]{0:T(256)S(1)}, f32[192]{0:T(256)}, u32[]{:S(2)}) copy-start(f32[192]{0:T(256)} %param.16) | copy-start | bytes 2308
  6.5 76.4 %all-gather.3.cloned.1.call-start = ((), (), s32[]{:S(2)}) async-start(), calls=%async_computation | async-start | bytes 4718592 | tf_op jit(solution)/shard_map/all_gather | solution.py:17
  10.9 16.3 %copy-start.16 = (s32[32,8]{0,1:T(8,128)S(1)}, s32[32,8]{0,1:T(8,128)}, u32[]{:S(2)}) copy-start(s32[32,8]{0,1:T(8,128)} %param.14) | copy-start | bytes 3076
  25.2 166.1 %all-gather.5.cloned.1.call-start = ((), (), s32[]{:S(2)}) async-start(), calls=%async_computation.1 | async-start | bytes 4718592 | tf_op jit(solution)/shard_map/all_gather | solution.py:17
  25.2 72.6 %collective-permute-start.2 = (bf16[2,1,16,16,192]{4,3,2,0,1:T(8,128)(2,1)S(1)}, bf16[2,1,16,16,192]{4,3,2,0,1:T(8,128)(2,1)S(1)}, u32[]{:S(2)}, u32[]{:S(2)}) collective-permute-start(bf16[2,1,16,16,192]{4,3,2,0,1:T(8,128)(2,1)S(1)} %slice.392), channel_id=1, source_target_pairs={{0,32},{32,64},{64,96},{96,128},{128,160},{160,192},{192,224},{1,3... | collective-permute-start | bytes 589832 | tf_op jit(solution)/shard_map/ppermute | solution.py:24
  85.3 10.1 %collective-permute-start = (bf16[2,1,4,192]{3,2,0,1:T(4,128)(2,1)S(1)}, bf16[2,1,4,192]{3,2,0,1:T(4,128)(2,1)S(1)}, u32[]{:S(2)}, u32[]{:S(2)}) collective-permute-start(bf16[2,1,4,192]{3,2,0,1:T(4,128)(2,1)S(1)} %slice.382), channel_id=1, source_target_pairs={{0,32},{32,64},{64,96},{96,128},{128,160},{160,192},{192,224},{1,3... | collective-permute-start | bytes 9224 | tf_op jit(solution)/shard_map/ppermute | solution.py:24
  91.9 5.6 %collective-permute-start.1 = (bf16[2,1,4,16,192]{4,3,0,2,1:T(8,128)(2,1)S(1)}, bf16[2,1,4,16,192]{4,3,0,2,1:T(8,128)(2,1)S(1)}, u32[]{:S(2)}, u32[]{:S(2)}) collective-permute-start(bf16[2,1,4,16,192]{4,3,0,2,1:T(8,128)(2,1)S(1)} %slice.385), channel_id=1, source_target_pairs={{0,32},{32,64},{64,96},{96,128},{128,160},{160,192},{192,224},{1,3... | collective-permute-start | bytes 147464 | tf_op jit(solution)/shard_map/ppermute | solution.py:24
  97.7 1.0 copy-start.17
  97.7 1.0 copy-start.20
  108.9 2.0 copy-start.13
  111.0 1.3 copy-start.11
  112.3 1.3 copy-start.9
  113.6 1.3 copy-start.7
  114.9 1.3 copy-start.5
  116.2 1.3 copy-start.3
  117.5 1.3 copy-start.1
  137.7 68.4 %collective-permute-start.5 = (bf16[2,1,16,16,192]{4,3,2,0,1:T(8,128)(2,1)S(1)}, bf16[2,1,16,16,192]{4,3,2,0,1:T(8,128)(2,1)S(1)}, u32[]{:S(2)}, u32[]{:S(2)}) collective-permute-start(bf16[2,1,16,16,192]{4,3,2,0,1:T(8,128)(2,1)S(1)} %slice_bitcast_fusion.36), channel_id=1, source_target_pairs={{0,32},{32,64},{64,96},{96,128},{128,160},{160,192},{192,224},{1,3... | collective-permute-start | bytes 589832 | tf_op jit(solution)/shard_map/ppermute | solution.py:24
  193.5 10.3 %collective-permute-start.3 = (bf16[2,1,4,192]{3,2,0,1:T(4,128)(2,1)S(1)}, bf16[2,1,4,192]{3,2,0,1:T(4,128)(2,1)S(1)}, u32[]{:S(2)}, u32[]{:S(2)}) collective-permute-start(bf16[2,1,4,192]{3,2,0,1:T(4,128)(2,1)S(1)} %slice.405), channel_id=1, source_target_pairs={{0,32},{32,64},{64,96},{96,128},{128,160},{160,192},{192,224},{1,3... | collective-permute-start | bytes 9224 | tf_op jit(solution)/shard_map/ppermute | solution.py:24
  200.1 5.6 %collective-permute-start.4 = (bf16[2,1,4,16,192]{4,3,0,2,1:T(8,128)(2,1)S(1)}, bf16[2,1,4,16,192]{4,3,0,2,1:T(8,128)(2,1)S(1)}, u32[]{:S(2)}, u32[]{:S(2)}) collective-permute-start(bf16[2,1,4,16,192]{4,3,0,2,1:T(8,128)(2,1)S(1)} %slice.408), channel_id=1, source_target_pairs={{0,32},{32,64},{64,96},{96,128},{128,160},{160,192},{192,224},{1,3... | collective-permute-start | bytes 147464 | tf_op jit(solution)/shard_map/ppermute | solution.py:24
  206.0 0.9 copy-start.19
  216.9 2.0 copy-start.14
  219.0 1.3 copy-start.12
  220.3 1.3 copy-start.10
  221.6 1.3 copy-start.8
  222.9 1.3 copy-start.6
  224.3 1.3 copy-start.4
  225.6 1.3 copy-start.2
  226.9 1.3 copy-start
  229.2 1.0 copy-start.15
Sparse Core Ops, SparseCore 0:
  25.3 57.6 all-gather.2
  137.8 53.3 all-gather.4
where the time goes:
time: 239 us; the launch traced here: 238 us
  waiting for transfers between devices  111 us (46%)
  local copies, waits for them, and re-layouts  36.9 us (15%)
  blocking collectives  27.9 us (12%)
  matrix products  26 us (11%)
  starting transfers between devices  14.9 us (6%)
  between operations  14.5 us (6%)
  other arithmetic  6.18 us (3%)
    all_gather x2, waiting for transfers between devices, gather_axes(): array = lax.all_gather(array, axis, axis=dim, tiled=True)  107 us
    all_gather x2, blocking collectives, gather_axes(): array = lax.all_gather(array, axis, axis=dim, tiled=True)  27.9 us
    dot_general x18, matrix products, conv_tile(): jnp.dot(window, weight[time_off * 3 + row_off], preferred_element_type=jn...  16.4 us
    ppermute x6, starting transfers between devices, shifted(): lax.ppermute(value, axis, [(source, source + steps) for source in range(f...  14.9 us
    cond x32, local copies, waits for them, and re-layouts  9.47 us
    dot_general x2, matrix products, fold_edges(): jnp.einsum('djn,fnjxc->fdjxc', side_choose, portion, preferred_element_ty...  9.26 us
    slice x2, local copies, waits for them, and re-layouts, conv_tile(): widened[time_off:time_off + frames_out, row_off:row_off + side_len]  8.72 us
    another operation x2, local copies, waits for them, and re-layouts  8.17 us
  transfers between devices with their start and end apart: 8, of which 4 were waited for; matrix products, arithmetic and copies ran while one was open for 6% of the time, Pallas kernels for 0%

commit v1 on v0

v1 whole, which is shorter than its diff:
```python
import functools

import jax
import jax.numpy as jnp
from jax import lax
from jax.experimental import pallas as pl
from jax.experimental.pallas import tpu as pltpu
from jax.sharding import PartitionSpec as P

EPS = 1e-06
BF = jnp.bfloat16
F32 = jnp.float32
NT = 32
TM = 8
C = 192
L = 2 * C


def chunk_of(dev):
    z, y = lax.div(dev, 4), lax.rem(dev, 4)
    strip = lax.rem(y, 2) * 2 + lax.div(y, 2)
    return strip * 8 + lax.rem(3 * (z + 16 - 2 * strip), 8)


def device_of(chunk):
    strip, low = chunk // 8, chunk % 8
    return ((3 * low + 2 * strip) % 8) * 4 + (strip % 2) * 2 + strip // 2


def lanes(shape):
    return lax.broadcasted_iota(jnp.int32, shape, len(shape) - 1)


def rows(shape):
    return lax.broadcasted_iota(jnp.int32, shape, len(shape) - 2)


def norm_silu(v, gain):
    sq = v * v
    low = lanes((v.shape[0], 128)) < 64
    mid = sq[:, 128:256]
    zero = jnp.zeros_like(mid)
    first = jnp.sum(sq[:, :128] + jnp.where(low, mid, zero), axis=-1, keepdims=True)
    second = jnp.sum(sq[:, 256:] + jnp.where(low, zero, mid), axis=-1, keepdims=True)
    first = lax.rsqrt(first * (1.0 / C) + EPS)
    second = lax.rsqrt(second * (1.0 / C) + EPS)
    y = v * jnp.where(lanes(v.shape) < C, first, second) * gain
    half = 0.5 * y
    return half + half * jnp.tanh(half)


def down(v, first_row):
    return jnp.where(rows(v.shape) == 0, first_row, pltpu.roll(v, 1, 0))


def up(v, last_row):
    n = v.shape[0]
    return jnp.where(rows(v.shape) == n - 1, last_row, pltpu.roll(v, n - 1, 0))


def kernel(
    video, nbr, vf, g1, w1, b1, g2, w2, b2, out,
    vid, wr1, wr2, wt1, wt2, act, strip32, snd, got1, snd2, got2, gotc,
    pact, psnd, pgot, pgotc, ring, acc, racc, hid, hring, phid, phring, obuf,
    lsem, s1, r1, s2, r2, sc, rc, st, rt,
):
    t, s = lax.axis_index("tm"), lax.axis_index("space")
    nxt, prv = lax.rem(t + 1, TM), lax.rem(t + TM - 1, TM)

    barrier = pltpu.get_barrier_semaphore()

    def greet(k, carry):
        pl.semaphore_signal(barrier, inc=1, device_id={"space": lax.rem(s + k, NT)})
        return carry

    lax.fori_loop(1, NT, greet, 0)
    pl.semaphore_signal(barrier, inc=1, device_id={"tm": nxt})
    pl.semaphore_signal(barrier, inc=1, device_id={"tm": prv})

    load_v = pltpu.make_async_copy(video.at[:, 0], vid, lsem.at[0])
    load_v.start()
    load_1 = pltpu.make_async_copy(w1, wr1, lsem.at[1])
    load_1.start()
    load_2 = pltpu.make_async_copy(w2, wr2, lsem.at[2])
    load_2.start()

    def twice(ref):
        one = ref[...].reshape(1, C)
        return jnp.concatenate([one, one], axis=1)

    gain1, bias1, gain2, bias2 = twice(g1), twice(b1), twice(g2), twice(b2)
    first_frame = 4 * t
    own_valid = vf[s]

    def valid_of(k):
        n = nbr[s, k]
        return jnp.where(n < NT, vf[jnp.minimum(n, NT - 1)], 0)

    near = [valid_of(k) for k in range(8)]
    zero_row = jnp.zeros((1, L), F32)

    load_v.wait()
    for f in range(4):
        there = first_frame + f < own_valid
        for m in range(8):
            a = norm_silu(vid[f, :, L * m : L * m + L].astype(F32), gain1)
            a = jnp.where(there, a, 0.0)
            act[1, m + 1, f + 2] = a.astype(BF)
            act[0, m + 1, f + 2] = down(a, zero_row).astype(BF)
            act[2, m + 1, f + 2] = up(a, zero_row).astype(BF)
            strip32[m, f : f + 1] = a[0:1]
            strip32[m, 4 + f : 5 + f] = a[1:2]
            strip32[8 + m, f : f + 1] = a[14:15]
            strip32[8 + m, 4 + f : 5 + f] = a[15:16]
            if m in (0, 7):
                base = (16 if m == 0 else 24) + 2 * f
                snd[base] = a[0:8].astype(BF)
                snd[base + 1] = a[8:16].astype(BF)
    for c in range(16):
        snd[c] = strip32[c].astype(BF)
    got1[NT] = jnp.zeros((8, L), BF)

    pl.semaphore_wait(barrier, NT + 1)

    def send_1(k):
        j = lax.rem(s + k, NT)
        return pltpu.make_async_remote_copy(
            snd.at[chunk_of(j)], got1.at[s], s1.at[k], r1.at[k], device_id={"space": j}
        )

    def start_1(k, carry):
        send_1(k).start()
        return carry

    lax.fori_loop(1, NT, start_1, 0)
    got1[s] = snd[chunk_of(s)]

    def to_next(i, src, dst):
        return pltpu.make_async_remote_copy(src, dst, st.at[i], rt.at[i], device_id={"tm": nxt})

    t_act = to_next(0, act.at[1, 1:9, 4:6], pact)
    t_act.start()
    t_snd = to_next(1, snd.at[0:16], psnd)
    t_snd.start()

    def toeplitz(i, raw, wide):
        zeros = jnp.zeros((C, C), BF)
        for b in range(4):
            left = raw[i, b * C : b * C + C] if b < 3 else zeros
            right = raw[i, b * C - C : b * C] if b > 0 else zeros
            wide[i, b * C : b * C + C] = jnp.concatenate([left, right], axis=1)

    load_1.wait()

    def widen_1(i, carry):
        toeplitz(i, wr1, wt1)
        return carry

    lax.fori_loop(0, 9, widen_1, 0)

    def recv_1(k, carry):
        i = lax.rem(s + NT - k, NT)
        pltpu.make_async_remote_copy(
            snd.at[0], got1.at[i], s1.at[k], r1.at[k], device_id={"space": i}
        ).wait_recv()
        return carry

    lax.fori_loop(1, NT, recv_1, 0)
    mine = chunk_of(s)
    strip = lax.div(mine, 8)
    side = jnp.where(strip == 0, 6, jnp.where(strip == 1, 1, jnp.where(strip == 2, 4, 3)))
    is_corner = (mine == 0) | (mine == 7) | (mine == 8) | (mine == 15)
    corner = lax.div(mine + 1, 4) - 2 * lax.div(mine, 8)
    corner = lax.div(corner, 2) + 2 * lax.div(mine, 8)
    corner = lax.rem(corner, 4)
    cside = jnp.where(mine == 0, 7, jnp.where(mine == 7, 5, jnp.where(mine == 8, 2, 0)))

    def pick(d, carry):
        snd2[0, d] = got1[nbr[d, side]]
        snd2[1, d] = got1[nbr[d, cside]]
        return carry

    lax.fori_loop(0, NT, pick, 0)

    def send_2(k):
        d = lax.rem(s + k, NT)
        return pltpu.make_async_remote_copy(
            snd2.at[0, d], got2.at[mine], s2.at[k], r2.at[k], device_id={"space": d}
        )

    def send_c(k):
        d = lax.rem(s + k, NT)
        return pltpu.make_async_remote_copy(
            snd2.at[1, d], gotc.at[corner], sc.at[k], rc.at[corner], device_id={"space": d}
        )

    def start_2(k, carry):
        send_2(k).start()
        return carry

    lax.fori_loop(1, NT, start_2, 0)
    got2[mine] = snd2[0, s]

    @pl.when(is_corner)
    def _():
        def start_c(k, carry):
            send_c(k).start()
            return carry

        lax.fori_loop(1, NT, start_c, 0)
        gotc[corner] = snd2[1, s]

    later = t > 0
    t_act.wait_recv()

    def before(m, carry):
        for f in range(2):
            a = jnp.where(later, pact[m, f].astype(F32), 0.0)
            act[1, m + 1, f] = a.astype(BF)
            act[0, m + 1, f] = down(a, zero_row).astype(BF)
            act[2, m + 1, f] = up(a, zero_row).astype(BF)
        return carry

    lax.fori_loop(0, 8, before, 0)

    total = jnp.zeros((7 * 64, L), F32)
    for p in range(3):
        for q in range(3):
            window = jnp.concatenate(
                [act[q, 1:8, p : p + 4].reshape(-1, L), act[q, 2:9, p : p + 4].reshape(-1, L)],
                axis=1,
            )
            total = total + jnp.dot(window, wt1[3 * p + q], preferred_element_type=F32)
    acc[1:8] = total.reshape(7, 4, 16, L)

    load_2.wait()

    def widen_2(i, carry):
        toeplitz(i, wr2, wt2)
        return carry

    lax.fori_loop(0, 9, widen_2, 0)

    def recv_2(k, carry):
        i = lax.rem(s + NT - k, NT)
        pltpu.make_async_remote_copy(
            snd2.at[0, 0], got2.at[chunk_of(i)], s2.at[k], r2.at[k], device_id={"space": i}
        ).wait_recv()
        return carry

    lax.fori_loop(1, NT, recv_2, 0)
    for i, c in enumerate((0, 7, 8, 15)):

        @pl.when(mine != c)
        def _():
            pltpu.make_async_remote_copy(
                snd2.at[1, 0], gotc.at[i], sc.at[0], rc.at[i], device_id={"space": device_of(c)}
            ).wait_recv()

    t_got = [
        to_next(2, got2.at[0:16], pgot.at[0:16]),
        to_next(3, got2.at[20:24], pgot.at[16:20]),
        to_next(4, got2.at[28:32], pgot.at[20:24]),
        to_next(5, gotc, pgotc),
    ]
    for copy in t_got:
        copy.start()

    def side_pair(m, f, pieces):
        a = jnp.concatenate([pieces[0], pieces[1]], axis=0)
        act[1, m, f] = a.astype(BF)
        act[0, m, f] = down(a, zero_row).astype(BF)
        act[2, m, f] = up(a, zero_row).astype(BF)
        return a

    r8 = rows((8, L))

    def keep(v):
        return jnp.where(later, v, 0.0)

    edges = {}
    for m, base in ((0, 24), (9, 16)):
        mixed = jnp.zeros((8, L), F32)
        for f in range(4):
            pieces = [got2[base + 2 * f + h].astype(F32) for h in range(2)]
            side_pair(m, f + 2, pieces)
            mixed = jnp.where(r8 == f, pieces[0][0:1], mixed)
            mixed = jnp.where(r8 == 4 + f, pieces[1][7:8], mixed)
        edges[m] = mixed
    for copy in t_got:
        copy.wait_recv()
    t_snd.wait_recv()
    pedges = {}
    for m, base in ((0, 20), (9, 16)):
        mixed = jnp.zeros((8, L), F32)
        for f in range(2):
            pieces = [keep(pgot[base + 2 * f + h].astype(F32)) for h in range(2)]
            side_pair(m, f, pieces)
            mixed = jnp.where(r8 == 2 + f, pieces[0][0:1], mixed)
            mixed = jnp.where(r8 == 6 + f, pieces[1][7:8], mixed)
        pedges[m] = mixed

    def at_frames(p, prev, own):
        if p == 2:
            return own
        n = 2 - p
        return jnp.where(lax.rem(r8, 4) < n, pltpu.roll(prev, 4 + n, 0), pltpu.roll(own, n, 0))

    upper = r8 < 4
    none = jnp.zeros((8, L), F32)

    def ring_rows(m, top, bottom, inner, ptop, pbottom, pinner):
        for p in range(3):
            xt = at_frames(p, ptop, top)
            xb = at_frames(p, pbottom, bottom)
            xo = at_frames(p, pinner, inner)
            xt4, xb4 = pltpu.roll(xt, 4, 0), pltpu.roll(xb, 4, 0)
            tiles = (
                (jnp.where(upper, xt, xo), jnp.where(upper, xt4, none)),
                (jnp.where(upper, xt4, xb4), none),
                (jnp.where(upper, xo, xb), jnp.where(upper, none, xb4)),
            )
            for q in range(3):
                ring[3 * p + q, m] = jnp.concatenate(tiles[q], axis=0).astype(BF)

    def wide(ref, i):
        return ref[i].astype(F32)

    def ring_pair(m, carry):
        inner = jnp.where(upper, wide(snd, m), wide(snd, 8 + m))
        pinner = keep(jnp.where(upper, wide(psnd, m), wide(psnd, 8 + m)))
        ring_rows(
            m + 1, wide(got2, 8 + m), wide(got2, m), inner,
            keep(wide(pgot, 8 + m)), keep(wide(pgot, m)), pinner,
        )
        return carry

    lax.fori_loop(0, 8, ring_pair, 0)
    ring_rows(
        0, wide(gotc, 3), wide(gotc, 1), edges[0],
        keep(wide(pgotc, 3)), keep(wide(pgotc, 1)), pedges[0],
    )
    ring_rows(
        9, wide(gotc, 2), wide(gotc, 0), edges[9],
        keep(wide(pgotc, 2)), keep(wide(pgotc, 0)), pedges[9],
    )

    total = jnp.zeros((2 * 64 + 9 * 16, L), F32)
    for p in range(3):
        for q in range(3):
            halves = []
            for d in range(2):
                halves.append(
                    jnp.concatenate(
                        [
                            act[q, d, p : p + 4].reshape(-1, L),
                            act[q, 8 + d, p : p + 4].reshape(-1, L),
                            ring[3 * p + q, d : d + 9].reshape(-1, L),
                        ],
                        axis=0,
                    )
                )
            window = jnp.concatenate(halves, axis=1)
            total = total + jnp.dot(window, wt1[3 * p + q], preferred_element_type=F32)
    acc[0] = total[0:64].reshape(4, 16, L)
    acc[8] = total[64:128].reshape(4, 16, L)
    racc[...] = total[128:].reshape(9, 16, L)

    def finish(m, carry):
        rim = racc[m]
        left_half = lanes((8, L)) < C

        def by_pair(left, middle, right):
            first = jnp.where(m == 0, left, middle)
            second = jnp.where(m == 8, right, middle)
            return first, second

        t0, t1 = by_pair(near[0], near[1], near[2])
        u0, u1 = by_pair(near[5], near[6], near[7])
        o0, o1 = by_pair(near[3], own_valid, near[4])
        limit = jnp.where(upper, jnp.where(left_half, t0, t1), jnp.where(left_half, u0, u1))
        outer = norm_silu(rim[0:8] + bias1, gain2)
        outer = jnp.where(first_frame + lax.rem(r8, 4) < limit, outer, 0.0)
        hring[m] = outer.astype(BF)
        limit = jnp.where(lanes((16, L)) < C, o0, o1)
        r16 = rows((16, L))
        for f in range(4):
            v = acc[m, f]
            v = v + jnp.where(r16 == 0, rim[8 + f : 9 + f], 0.0)
            v = v + jnp.where(r16 == 15, rim[12 + f : 13 + f], 0.0)
            h = norm_silu(v + bias1, gain2)
            h = jnp.where(first_frame + f < limit, h, 0.0)
            hid[1, m, f + 2] = h.astype(BF)
            hid[0, m, f + 2] = down(h, outer[f : f + 1]).astype(BF)
            hid[2, m, f + 2] = up(h, outer[4 + f : 5 + f]).astype(BF)
        return carry

    lax.fori_loop(0, 9, finish, 0)
    t_hid = [to_next(6, hid.at[1, :, 4:6], phid), to_next(7, hring, phring)]
    for copy in t_hid:
        copy.start()

    def conv2(half):
        total = jnp.zeros((8 * 32, L), F32)
        for p in range(3):
            for q in range(3):
                f = 2 * half + p
                window = jnp.concatenate(
                    [hid[q, 0:8, f : f + 2].reshape(-1, L), hid[q, 1:9, f : f + 2].reshape(-1, L)],
                    axis=1,
                )
                total = total + jnp.dot(window, wt2[3 * p + q], preferred_element_type=F32)
        total = total.reshape(8, 2, 16, L)
        for g in range(2):
            f = 2 * half + g
            there = first_frame + f < own_valid
            for m in range(8):
                x = vid[f, :, L * m : L * m + L].astype(F32)
                o = jnp.where(there, total[m, g] + bias2 + x, 0.0)
                obuf[f, :, L * m : L * m + L] = o.astype(BF)
        copy = pltpu.make_async_copy(
            obuf.at[2 * half : 2 * half + 2], out.at[2 * half : 2 * half + 2, 0], lsem.at[3 + half]
        )
        copy.start()
        return copy

    store_1 = conv2(1)
    for copy in t_hid:
        copy.wait_recv()

    def before_2(m, carry):
        rim = keep(phring[m].astype(F32))
        for f in range(2):
            h = keep(phid[m, f].astype(F32))
            hid[1, m, f] = h.astype(BF)
            hid[0, m, f] = down(h, rim[2 + f : 3 + f]).astype(BF)
            hid[2, m, f] = up(h, rim[6 + f : 7 + f]).astype(BF)
        return carry

    lax.fori_loop(0, 9, before_2, 0)
    store_0 = conv2(0)

    def sent(k, carry):
        send_1(k).wait_send()
        send_2(k).wait_send()
        return carry

    lax.fori_loop(1, NT, sent, 0)

    @pl.when(is_corner)
    def _():
        def sent_c(k, carry):
            send_c(k).wait_send()
            return carry

        lax.fori_loop(1, NT, sent_c, 0)

    for copy in [t_act, t_snd, *t_got, *t_hid]:
        copy.wait_send()
    store_1.wait()
    store_0.wait()


def on_device(video, nbr, vf, g1, w1, b1, g2, w2, b2):
    vmem = lambda *shape, dtype=BF: pltpu.VMEM(shape, dtype)
    dma = lambda n: pltpu.SemaphoreType.DMA((n,))
    hbm = pl.BlockSpec(memory_space=pl.ANY)
    smem = pl.BlockSpec(memory_space=pltpu.SMEM)
    local = pl.BlockSpec(memory_space=pltpu.VMEM)
    return pl.pallas_call(
        kernel,
        out_shape=jax.ShapeDtypeStruct(video.shape, BF),
        in_specs=[hbm, smem, smem, local, hbm, local, local, hbm, local],
        out_specs=hbm,
        scratch_shapes=[
            vmem(4, 16, 16 * C),
            vmem(9, 3 * C, C),
            vmem(9, 3 * C, C),
            vmem(9, 4 * C, L),
            vmem(9, 4 * C, L),
            vmem(3, 10, 6, 16, L),
            vmem(16, 8, L, dtype=F32),
            vmem(32, 8, L),
            vmem(NT + 1, 8, L),
            vmem(2, NT, 8, L),
            vmem(32, 8, L),
            vmem(4, 8, L),
            vmem(8, 2, 16, L),
            vmem(16, 8, L),
            vmem(24, 8, L),
            vmem(4, 8, L),
            vmem(9, 10, 16, L),
            vmem(9, 4, 16, L, dtype=F32),
            vmem(9, 16, L, dtype=F32),
            vmem(3, 9, 6, 16, L),
            vmem(9, 8, L),
            vmem(9, 2, 16, L),
            vmem(9, 8, L),
            vmem(4, 16, 16 * C),
            dma(5), dma(NT), dma(NT), dma(NT), dma(NT), dma(NT), dma(4), dma(8), dma(8),
        ],
        compiler_params=pltpu.CompilerParams(
            collective_id=0, has_side_effects=True, vmem_limit_bytes=60 * 1024 * 1024
        ),
    )(video, nbr, vf, g1, w1, b1, g2, w2, b2)


def solution(mesh):
    placed = (P("tm", "space", None, None), P(), P(), P(), P(), P(), P(), P(), P())
    return jax.shard_map(
        on_device, mesh=mesh, in_specs=placed, out_specs=P("tm", "space", None, None), check_vma=False
    )
```

time: 239 us -> 55.8 us (0.23)
  the two profiles are of different devices: /device:TPU:2 before, /device:TPU:8 now
where the time goes in v1:
time: 55.8 us; the launch traced here: 55.5 us
  Pallas kernels  43.9 us (79%)
  local copies, waits for them, and re-layouts  11.6 us (21%)
    pallas_call x1, Pallas kernels, on_device(): pl.pallas_call(kernel, out_shape=jax.ShapeDtypeStruct(video.shape, BF), i...  43.9 us
    unnamed x6, local copies, waits for them, and re-layouts  11.6 us

profile of v1, /device:TPU:8, one launch (start us, length us, event | category | flops | bytes accessed | tf_op | source)
XLA Modules:
  0.0 55.5 jit_solution(10412550743745414021)
XLA Ops:
  0.0 0.0 copy-start
  0.0 1.5 %copy.10.nbr = s32[32,8]{1,0:T(8,128)} copy(s32[32,8]{0,1:T(8,128)} %param.10) | data formatting | bytes 2048 | tf_op args[1]
  1.5 4.5 %copy.11.w1 = bf16[9,576,192]{2,1,0:T(8,128)(2,1)} copy(bf16[9,576,192]{1,2,0:T(8,128)(2,1)} %param.13) | data formatting | bytes 3981312 | tf_op args[4]
  6.1 0.0 copy-done
  6.1 3.8 %copy.12.w2 = bf16[9,576,192]{2,1,0:T(8,128)(2,1)} copy(bf16[9,576,192]{1,2,0:T(8,128)(2,1)S(1)} %copy-done) | data formatting | bytes 3981312 | tf_op args[7]
  9.9 43.9 %shard_map.91 = bf16[4,1,16,3072]{3,2,1,0:T(8,128)(2,1)} custom-call(bf16[4,1,16,3072]{3,2,1,0:T(8,128)(2,1)} %video.1, s32[32,8]{1,0:T(8,128)} %copy.10.nbr, s32[32]{0:T(128)} %vf.1, f32[192]{0:T(256)} %g1.1, bf16[9,576,192]{2,1,0:T(8,128)(2,1)} %copy.11.w1, f32[192]{0:T(256)} %b1.1, f32[192]{0:T(256)} %g2.1, bf16[9,576,192]{2,1,0:T(8,128)(2,1)} %copy.12.w2, ...), custom_call_target="tpu_custom_call" | custom-call | tf_op jit(solution)/shard_map/pallas_call | solution.py:470
  53.7 1.8 %copy.14 = bf16[4,1,16,3072]{3,2,1,0:T(8,128)(2,1)} copy(bf16[4,1,16,3072]{3,2,1,0:T(8,128)(2,1)} %shard_map.91) | data formatting | bytes 786432
Async XLA Ops:
  0.0 6.1 %copy-start = (bf16[9,576,192]{1,2,0:T(8,128)(2,1)S(1)}, bf16[9,576,192]{1,2,0:T(8,128)(2,1)}, u32[]{:S(2)}) copy-start(bf16[9,576,192]{1,2,0:T(8,128)(2,1)} %param.16) | copy-start | bytes 5971972

commit v2 on v1

--- a/solution.py
+++ b/solution.py
@@ -49,6 +49,10 @@
     return half + half * jnp.tanh(half)
 
 
+def matmul(a, b):
+    return lax.dot_general(a, b, (((1,), (1,)), ((), ())), preferred_element_type=F32)
+
+
 def down(v, first_row):
     return jnp.where(rows(v.shape) == 0, first_row, pltpu.roll(v, 1, 0))
 
@@ -59,9 +63,9 @@
 
 
 def kernel(
-    video, nbr, vf, g1, w1, b1, g2, w2, b2, out,
-    vid, wr1, wr2, wt1, wt2, act, strip32, snd, got1, snd2, got2, gotc,
-    pact, psnd, pgot, pgotc, ring, acc, racc, hid, hring, phid, phring, obuf,
+    video, nbr_in, vf_in, g1_in, w1, b1_in, g2_in, w2, b2_in, out,
+    nbr, vf, g1, b1, g2, b2, vid, wr1, wr2, wt1, wt2, act, strip32, snd, got1, snd2, got2, gotc,
+    pact, psnd, pgot, pgotc, ring, acc, racc, hid, hring, phid, phring,
     lsem, s1, r1, s2, r2, sc, rc, st, rt,
 ):
     t, s = lax.axis_index("tm"), lax.axis_index("space")
@@ -77,6 +81,14 @@
     pl.semaphore_signal(barrier, inc=1, device_id={"tm": nxt})
     pl.semaphore_signal(barrier, inc=1, device_id={"tm": prv})
 
+    loads = [
+        pltpu.make_async_copy(src, dst, lsem.at[3 + i])
+        for i, (src, dst) in enumerate(
+            ((nbr_in, nbr), (vf_in, vf), (g1_in, g1), (b1_in, b1), (g2_in, g2), (b2_in, b2))
+        )
+    ]
+    for copy in loads:
+        copy.start()
     load_v = pltpu.make_async_copy(video.at[:, 0], vid, lsem.at[0])
     load_v.start()
     load_1 = pltpu.make_async_copy(w1, wr1, lsem.at[1])
@@ -84,6 +96,9 @@
     load_2 = pltpu.make_async_copy(w2, wr2, lsem.at[2])
     load_2.start()
 
+    for copy in loads:
+        copy.wait()
+
     def twice(ref):
         one = ref[...].reshape(1, C)
         return jnp.concatenate([one, one], axis=1)
@@ -93,7 +108,7 @@
     own_valid = vf[s]
 
     def valid_of(k):
-        n = nbr[s, k]
+        n = nbr[k, s]
         return jnp.where(n < NT, vf[jnp.minimum(n, NT - 1)], 0)
 
     near = [valid_of(k) for k in range(8)]
@@ -145,10 +160,9 @@
 
     def toeplitz(i, raw, wide):
         zeros = jnp.zeros((C, C), BF)
-        for b in range(4):
-            left = raw[i, b * C : b * C + C] if b < 3 else zeros
-            right = raw[i, b * C - C : b * C] if b > 0 else zeros
-            wide[i, b * C : b * C + C] = jnp.concatenate([left, right], axis=1)
+        one = raw[i]
+        wide[i, 0:C] = jnp.concatenate([one, zeros], axis=1)
+        wide[i, C:L] = jnp.concatenate([zeros, one], axis=1)
 
     load_1.wait()
 
@@ -170,14 +184,12 @@
     strip = lax.div(mine, 8)
     side = jnp.where(strip == 0, 6, jnp.where(strip == 1, 1, jnp.where(strip == 2, 4, 3)))
     is_corner = (mine == 0) | (mine == 7) | (mine == 8) | (mine == 15)
-    corner = lax.div(mine + 1, 4) - 2 * lax.div(mine, 8)
-    corner = lax.div(corner, 2) + 2 * lax.div(mine, 8)
-    corner = lax.rem(corner, 4)
+    corner = lax.rem(2 * strip + lax.div(lax.rem(mine, 8), 7), 4)
     cside = jnp.where(mine == 0, 7, jnp.where(mine == 7, 5, jnp.where(mine == 8, 2, 0)))
 
     def pick(d, carry):
-        snd2[0, d] = got1[nbr[d, side]]
-        snd2[1, d] = got1[nbr[d, cside]]
+        snd2[0, d] = got1[nbr[side, d]]
+        snd2[1, d] = got1[nbr[cside, d]]
         return carry
 
     lax.fori_loop(0, NT, pick, 0)
@@ -230,7 +242,7 @@
                 [act[q, 1:8, p : p + 4].reshape(-1, L), act[q, 2:9, p : p + 4].reshape(-1, L)],
                 axis=1,
             )
-            total = total + jnp.dot(window, wt1[3 * p + q], preferred_element_type=F32)
+            total = total + matmul(window, wt1[3 * p + q])
     acc[1:8] = total.reshape(7, 4, 16, L)
 
     load_2.wait()
@@ -361,7 +373,7 @@
                     )
                 )
             window = jnp.concatenate(halves, axis=1)
-            total = total + jnp.dot(window, wt1[3 * p + q], preferred_element_type=F32)
+            total = total + matmul(window, wt1[3 * p + q])
     acc[0] = total[0:64].reshape(4, 16, L)
     acc[8] = total[64:128].reshape(4, 16, L)
     racc[...] = total[128:].reshape(9, 16, L)
@@ -409,7 +421,7 @@
                     [hid[q, 0:8, f : f + 2].reshape(-1, L), hid[q, 1:9, f : f + 2].reshape(-1, L)],
                     axis=1,
                 )
-                total = total + jnp.dot(window, wt2[3 * p + q], preferred_element_type=F32)
+                total = total + matmul(window, wt2[3 * p + q])
         total = total.reshape(8, 2, 16, L)
         for g in range(2):
             f = 2 * half + g
@@ -417,14 +429,9 @@
             for m in range(8):
                 x = vid[f, :, L * m : L * m + L].astype(F32)
                 o = jnp.where(there, total[m, g] + bias2 + x, 0.0)
-                obuf[f, :, L * m : L * m + L] = o.astype(BF)
-        copy = pltpu.make_async_copy(
-            obuf.at[2 * half : 2 * half + 2], out.at[2 * half : 2 * half + 2, 0], lsem.at[3 + half]
-        )
-        copy.start()
-        return copy
-
-    store_1 = conv2(1)
+                out[f, 0, :, L * m : L * m + L] = o.astype(BF)
+
+    conv2(1)
     for copy in t_hid:
         copy.wait_recv()
 
@@ -438,7 +445,7 @@
         return carry
 
     lax.fori_loop(0, 9, before_2, 0)
-    store_0 = conv2(0)
+    conv2(0)
 
     def sent(k, carry):
         send_1(k).wait_send()
@@ -457,27 +464,27 @@
 
     for copy in [t_act, t_snd, *t_got, *t_hid]:
         copy.wait_send()
-    store_1.wait()
-    store_0.wait()
 
 
 def on_device(video, nbr, vf, g1, w1, b1, g2, w2, b2):
     vmem = lambda *shape, dtype=BF: pltpu.VMEM(shape, dtype)
     dma = lambda n: pltpu.SemaphoreType.DMA((n,))
-    hbm = pl.BlockSpec(memory_space=pl.ANY)
-    smem = pl.BlockSpec(memory_space=pltpu.SMEM)
+    hbm = pl.BlockSpec(memory_space=pltpu.HBM)
     local = pl.BlockSpec(memory_space=pltpu.VMEM)
     return pl.pallas_call(
         kernel,
-        out_shape=jax.ShapeDtypeStruct(video.shape, BF),
-        in_specs=[hbm, smem, smem, local, hbm, local, local, hbm, local],
-        out_specs=hbm,
+        out_shape=pltpu.VMEM(video.shape, BF),
+        in_specs=[hbm] * 9,
+        out_specs=local,
         scratch_shapes=[
+            pltpu.SMEM((8, NT), jnp.int32),
+            pltpu.SMEM((NT,), jnp.int32),
+            *[vmem(C, dtype=F32)] * 4,
             vmem(4, 16, 16 * C),
-            vmem(9, 3 * C, C),
-            vmem(9, 3 * C, C),
-            vmem(9, 4 * C, L),
-            vmem(9, 4 * C, L),
+            vmem(9, C, 3 * C),
+            vmem(9, C, 3 * C),
+            vmem(9, L, 4 * C),
+            vmem(9, L, 4 * C),
             vmem(3, 10, 6, 16, L),
             vmem(16, 8, L, dtype=F32),
             vmem(32, 8, L),
@@ -496,13 +503,12 @@
             vmem(9, 8, L),
             vmem(9, 2, 16, L),
             vmem(9, 8, L),
-            vmem(4, 16, 16 * C),
-            dma(5), dma(NT), dma(NT), dma(NT), dma(NT), dma(NT), dma(4), dma(8), dma(8),
+            dma(9), dma(NT), dma(NT), dma(NT), dma(NT), dma(NT), dma(4), dma(8), dma(8),
         ],
         compiler_params=pltpu.CompilerParams(
-            collective_id=0, has_side_effects=True, vmem_limit_bytes=60 * 1024 * 1024
+            collective_id=0, has_side_effects=True, vmem_limit_bytes=66000000
         ),
-    )(video, nbr, vf, g1, w1, b1, g2, w2, b2)
+    )(video, nbr.T, vf, g1, jnp.swapaxes(w1, 1, 2), b1, g2, jnp.swapaxes(w2, 1, 2), b2)
 
 
 def solution(mesh):

time: 55.8 us -> 43.1 us (0.77)
  local copies, waits for them, and re-layouts: 11.6 us -> 0.75 us
  Pallas kernels: 43.9 us -> 42.2 us
    unnamed x6 -> x1, local copies, waits for them, and re-layouts: 11.6 us -> 0.75 us
    pallas_call x1, Pallas kernels: 43.9 us -> 42.2 us  [on_device(): pl.pallas_call(kernel, out_shape=pltpu.VMEM(video.shape, BF), in_specs=[h...]
where the time goes in v2:
time: 43.1 us; the launch traced here: 43 us
  Pallas kernels  42.2 us (98%)
  local copies, waits for them, and re-layouts  0.75 us (2%)
    pallas_call x1, Pallas kernels, on_device(): pl.pallas_call(kernel, out_shape=pltpu.VMEM(video.shape, BF), in_specs=[h...  42.2 us

profile of v2, /device:TPU:8, one launch (start us, length us, event | category | flops | bytes accessed | tf_op | source)
XLA Modules:
  0.0 43.0 jit_solution(18122764366485649844)
XLA Ops:
  0.0 42.2 %shard_map.91 = bf16[4,1,16,3072]{3,2,1,0:T(8,128)(2,1)S(1)} custom-call(bf16[4,1,16,3072]{3,2,1,0:T(8,128)(2,1)} %video.1, s32[8,32]{1,0:T(8,128)} %bitcast.5, s32[32]{0:T(128)} %vf_in.1, f32[192]{0:T(256)} %g1_in.1, bf16[9,192,576]{2,1,0:T(8,128)(2,1)} %bitcast.3, f32[192]{0:T(256)} %b1_in.1, f32[192]{0:T(256)} %g2_in.1, bf16[9,192,576]{2,1,0:T(8,128)(2,1)} %bitcast.4, ...), custom_call_target="tpu_custom_call" | custom-call | tf_op jit(solution)/shard_map/pallas_call | solution.py:474
  42.3 0.7 %copy.11 = bf16[4,1,16,3072]{3,2,1,0:T(8,128)(2,1)} copy(bf16[4,1,16,3072]{3,2,1,0:T(8,128)(2,1)S(1)} %shard_map.91) | data formatting | bytes 786432

commit v3 on v2

v3 whole, which is shorter than its diff:
```python
import functools

import jax
import jax.numpy as jnp
from jax import lax
from jax.experimental import pallas as pl
from jax.experimental.pallas import tpu as pltpu
from jax.sharding import PartitionSpec as P

EPS = 1e-06
BF = jnp.bfloat16
F32 = jnp.float32
NT = 32
TM = 8
C = 192
L = 2 * C


def chunk_of(dev):
    z, y = lax.div(dev, 4), lax.rem(dev, 4)
    strip = lax.rem(y, 2) * 2 + lax.div(y, 2)
    return strip * 8 + lax.rem(3 * (z + 16 - 2 * strip), 8)


def device_of(chunk):
    strip, low = chunk // 8, chunk % 8
    return ((3 * low + 2 * strip) % 8) * 4 + (strip % 2) * 2 + strip // 2


def offset(i):
    return 16 + (1 - 2 * lax.rem(i, 2)) * lax.div(i + 1, 2)


def lanes(shape):
    return lax.broadcasted_iota(jnp.int32, shape, len(shape) - 1)


def rows(shape):
    return lax.broadcasted_iota(jnp.int32, shape, len(shape) - 2)


def norm_silu(v, gain):
    sq = v * v
    low = lanes((v.shape[0], 128)) < 64
    mid = sq[:, 128:256]
    zero = jnp.zeros_like(mid)
    first = jnp.sum(sq[:, :128] + jnp.where(low, mid, zero), axis=-1, keepdims=True)
    second = jnp.sum(sq[:, 256:] + jnp.where(low, zero, mid), axis=-1, keepdims=True)
    first = lax.rsqrt(first * (1.0 / C) + EPS)
    second = lax.rsqrt(second * (1.0 / C) + EPS)
    y = v * jnp.where(lanes(v.shape) < C, first, second) * gain
    half = 0.5 * y
    return half + half * jnp.tanh(half)


def matmul(a, b):
    return lax.dot_general(a, b, (((1,), (1,)), ((), ())), preferred_element_type=F32)


def conv_rows(windows, near_w, far_w):
    first = jnp.concatenate([w[:, : C + L + 64] for w in windows], axis=1)
    second = jnp.concatenate([w[:, 128:] for w in windows], axis=1)
    near_w = jnp.concatenate([near_w[i] for i in range(9)], axis=1)
    far_w = jnp.concatenate([far_w[i] for i in range(9)], axis=1)
    a, b = matmul(first, near_w), matmul(second, far_w)
    return jnp.concatenate([a[:, :128], a[:, 128:] + b[:, :128], b[:, 128:]], axis=1)


def down(v, first_row):
    return jnp.where(rows(v.shape) == 0, first_row, pltpu.roll(v, 1, 0))


def up(v, last_row):
    n = v.shape[0]
    return jnp.where(rows(v.shape) == n - 1, last_row, pltpu.roll(v, n - 1, 0))


def kernel(
    video, nbr_in, vf_in, g1_in, w1, b1_in, g2_in, w2, b2_in, out,
    nbr, vf, g1, b1, g2, b2, vid, wr1, wr2, near1, far1, near2, far2, act, strip32, snd, got1, snd2, got2,
    pact, psnd, pgot, inner, pinner, ring, acc, racc, hid, hring, phid, phring,
    lsem, s1, r1, s2, r2, sc, rc, st, rt,
):
    t, s = lax.axis_index("tm"), lax.axis_index("space")
    nxt, prv = lax.rem(t + 1, TM), lax.rem(t + TM - 1, TM)

    barrier = pltpu.get_barrier_semaphore()

    later, sends = t > 0, t < TM - 1

    def greet(i, carry):
        pl.semaphore_signal(barrier, inc=1, device_id={"space": lax.rem(s + offset(i), NT)})
        return carry

    lax.fori_loop(0, NT - 1, greet, 0)

    @pl.when(sends)
    def _():
        pl.semaphore_signal(barrier, inc=1, device_id={"tm": nxt})

    @pl.when(later)
    def _():
        pl.semaphore_signal(barrier, inc=1, device_id={"tm": prv})

    loads = [
        pltpu.make_async_copy(src, dst, lsem.at[3 + i])
        for i, (src, dst) in enumerate(
            ((nbr_in, nbr), (vf_in, vf), (g1_in, g1), (b1_in, b1), (g2_in, g2), (b2_in, b2))
        )
    ]
    for copy in loads:
        copy.start()
    load_v = pltpu.make_async_copy(video.at[:, 0], vid, lsem.at[0])
    load_v.start()
    load_1 = pltpu.make_async_copy(w1, wr1, lsem.at[1])
    load_1.start()
    load_2 = pltpu.make_async_copy(w2, wr2, lsem.at[2])
    load_2.start()

    for copy in loads:
        copy.wait()

    def twice(ref):
        one = ref[...].reshape(1, C)
        return jnp.concatenate([one, one], axis=1)

    gain1, bias1, gain2, bias2 = twice(g1), twice(b1), twice(g2), twice(b2)
    first_frame = 4 * t
    own_valid = vf[s]

    def valid_of(k):
        n = nbr[k, s]
        return jnp.where(n < NT, vf[jnp.minimum(n, NT - 1)], 0)

    near = [valid_of(k) for k in range(8)]
    zero_row = jnp.zeros((1, L), F32)

    load_v.wait()
    for f in range(4):
        there = first_frame + f < own_valid
        for m in range(8):
            a = norm_silu(vid[f, :, L * m : L * m + L].astype(F32), gain1)
            a = jnp.where(there, a, 0.0)
            act[1, m + 1, f + 2] = a.astype(BF)
            act[0, m + 1, f + 2] = down(a, zero_row).astype(BF)
            act[2, m + 1, f + 2] = up(a, zero_row).astype(BF)
            strip32[m, f : f + 1] = a[0:1]
            strip32[m, 4 + f : 5 + f] = a[1:2]
            strip32[8 + m, f : f + 1] = a[14:15]
            strip32[8 + m, 4 + f : 5 + f] = a[15:16]
            if m in (0, 7):
                base = (16 if m == 0 else 24) + 2 * f
                snd[base] = a[0:8].astype(BF)
                snd[base + 1] = a[8:16].astype(BF)
    for c in range(16):
        snd[c] = strip32[c].astype(BF)
    got1[NT] = jnp.zeros((8, L), BF)

    pl.semaphore_wait(barrier, NT - 1 + jnp.where(later, 1, 0) + jnp.where(sends, 1, 0))

    def send_1(k):
        j = lax.rem(s + k, NT)
        return pltpu.make_async_remote_copy(
            snd.at[chunk_of(j)], got1.at[s], s1.at[k], r1.at[k], device_id={"space": j}
        )

    def start_1(i, carry):
        send_1(offset(i)).start()
        return carry

    lax.fori_loop(0, NT - 1, start_1, 0)
    got1[s] = snd[chunk_of(s)]

    def to_next(i, src, dst):
        return pltpu.make_async_remote_copy(src, dst, st.at[i], rt.at[i], device_id={"tm": nxt})

    t_act = to_next(0, act.at[1, 1:9, 4:6], pact)
    t_snd = to_next(1, snd.at[0:16], psnd)

    @pl.when(sends)
    def _():
        t_act.start()
        t_snd.start()

    def widen(i, raw, near_w, far_w):
        one, pad = raw[i], jnp.zeros((C, 64), BF)
        near_w[i, 0:C] = jnp.concatenate([one, pad], axis=1)
        near_w[i, C:256] = jnp.zeros((64, C + L + 64), BF)
        far_w[i, 0:64] = jnp.zeros((64, C + L + 64), BF)
        far_w[i, 64:256] = jnp.concatenate([pad, one], axis=1)

    load_1.wait()

    def widen_1(i, carry):
        widen(i, wr1, near1, far1)
        return carry

    lax.fori_loop(0, 9, widen_1, 0)

    def recv_1(k, carry):
        i = lax.rem(s + NT - k, NT)
        pltpu.make_async_remote_copy(
            snd.at[0], got1.at[i], s1.at[k], r1.at[k], device_id={"space": i}
        ).wait_recv()
        return carry

    lax.fori_loop(1, NT, recv_1, 0)
    mine = chunk_of(s)
    strip = lax.div(mine, 8)
    side = jnp.where(strip == 0, 6, jnp.where(strip == 1, 1, jnp.where(strip == 2, 4, 3)))
    is_corner = (mine == 0) | (mine == 7) | (mine == 8) | (mine == 15)
    slot_of = lambda c: c + 1 + 2 * jnp.minimum(lax.div(c, 8), 1) + lax.div(c, 16)
    slot = slot_of(mine)
    corner = jnp.minimum(10 * strip + 9 * (1 - lax.div(lax.rem(mine, 8), 7)), 19)
    cside = jnp.where(mine == 0, 7, jnp.where(mine == 7, 5, jnp.where(mine == 8, 2, 0)))

    def pick(d, carry):
        snd2[0, d] = got1[nbr[side, d]]
        snd2[1, d] = got1[nbr[cside, d]]
        return carry

    lax.fori_loop(0, NT, pick, 0)

    def send_2(k):
        d = lax.rem(s + k, NT)
        return pltpu.make_async_remote_copy(
            snd2.at[0, d], got2.at[slot], s2.at[k], r2.at[k], device_id={"space": d}
        )

    def send_c(k):
        d = lax.rem(s + k, NT)
        return pltpu.make_async_remote_copy(
            snd2.at[1, d], got2.at[corner], sc.at[k], rc.at[corner], device_id={"space": d}
        )

    def start_2(i, carry):
        k = offset(i)
        send_2(k).start()

        @pl.when(is_corner)
        def _():
            send_c(k).start()

        return carry

    lax.fori_loop(0, NT - 1, start_2, 0)
    got2[slot] = snd2[0, s]

    @pl.when(is_corner)
    def _():
        got2[corner] = snd2[1, s]

    @pl.when(later)
    def _():
        t_act.wait_recv()

    def before(m, carry):
        for f in range(2):
            a = jnp.where(later, pact[m, f].astype(F32), 0.0)
            act[1, m + 1, f] = a.astype(BF)
            act[0, m + 1, f] = down(a, zero_row).astype(BF)
            act[2, m + 1, f] = up(a, zero_row).astype(BF)
        return carry

    lax.fori_loop(0, 8, before, 0)

    windows = []
    for p in range(3):
        for q in range(3):
            windows.append(
                jnp.concatenate(
                    [act[q, 1:8, p : p + 4].reshape(-1, L), act[q, 2:9, p : p + 4].reshape(-1, L)],
                    axis=1,
                )
            )
    acc[1:8] = conv_rows(windows, near1, far1).reshape(7, 4, 16, L)

    load_2.wait()

    def widen_2(i, carry):
        widen(i, wr2, near2, far2)
        return carry

    lax.fori_loop(0, 9, widen_2, 0)

    def recv_2(k, carry):
        i = lax.rem(s + NT - k, NT)
        pltpu.make_async_remote_copy(
            snd2.at[0, 0], got2.at[slot_of(chunk_of(i))], s2.at[k], r2.at[k], device_id={"space": i}
        ).wait_recv()
        return carry

    lax.fori_loop(1, NT, recv_2, 0)
    for place, c in ((9, 0), (0, 7), (19, 8), (10, 15)):

        @pl.when(mine != c)
        def _():
            pltpu.make_async_remote_copy(
                snd2.at[1, 0], got2.at[place], sc.at[0], rc.at[place],
                device_id={"space": device_of(c)},
            ).wait_recv()

    t_got = [
        to_next(2, got2.at[0:20], pgot.at[0:20]),
        to_next(3, got2.at[24:28], pgot.at[20:24]),
        to_next(4, got2.at[32:36], pgot.at[24:28]),
    ]

    @pl.when(sends)
    def _():
        for copy in t_got:
            copy.start()

    r8 = rows((8, L))
    upper = r8 < 4

    def keep(v):
        return jnp.where(later, v, 0.0)

    def wide(ref, i):
        return ref[i].astype(F32)

    def side_pair(m, f, pieces):
        a = jnp.concatenate(pieces, axis=0)
        act[1, m, f] = a.astype(BF)
        act[0, m, f] = down(a, zero_row).astype(BF)
        act[2, m, f] = up(a, zero_row).astype(BF)

    def side_pairs(ref, bases, first, count, into, clean):
        for m, base in zip((0, 9), bases):
            mixed = jnp.zeros((8, L), F32)
            for f in range(4 - count, 4):
                at = base + 2 * (f - 4 + count)
                pieces = [clean(wide(ref, at)), clean(wide(ref, at + 1))]
                side_pair(m, first + f - 4 + count, pieces)
                mixed = jnp.where(r8 == f, pieces[0][0:1], mixed)
                mixed = jnp.where(r8 == 4 + f, pieces[1][7:8], mixed)
            into[m] = mixed

    side_pairs(got2, (28, 20), 2, 4, inner, lambda v: v)
    for m in range(8):
        inner[m + 1] = jnp.where(upper, wide(snd, m), wide(snd, 8 + m))

    def two_frames(half, p, own, prev):
        if half == 1:
            return pltpu.roll(own, 8 - p, 0) if p else own
        if p == 2:
            return own
        if p == 0:
            return pltpu.roll(prev, 6, 0)
        return jnp.where(lax.rem(r8, 4) == 0, pltpu.roll(prev, 5, 0), pltpu.roll(own, 1, 0))

    duo = lax.div(r8, 2)
    none = jnp.zeros((8, L), F32)

    def ring_tiles(half, m):
        own = [wide(got2, 10 + m), wide(got2, m), inner[m]]
        prev = own
        if half == 0:
            prev = [keep(wide(pgot, 10 + m)), keep(wide(pgot, m)), pinner[m]]
        tiles = {}
        for p in range(3):
            t0, b0, o0 = [two_frames(half, p, a, b) for a, b in zip(own, prev)]
            b6 = pltpu.roll(b0, 6, 0)
            low = jnp.where(duo == 1, pltpu.roll(o0, 6, 0), jnp.where(duo == 3, none, t0))
            mid = jnp.where(duo == 0, pltpu.roll(t0, 4, 0), jnp.where(duo == 1, pltpu.roll(b0, 2, 0), none))
            top = jnp.where(duo == 0, o0, jnp.where(duo == 2, none, b6))
            for q, tile in enumerate((low, mid, top)):
                tiles[3 * p + q] = tile.astype(BF)
        return tiles

    for i in range(9):
        ring[1, i, 5, 8:16] = none.astype(BF)

    def rim(half):
        def pairs(u, carry):
            even, odd = ring_tiles(half, 2 * u), ring_tiles(half, 2 * u + 1)
            for i in range(9):
                ring[0, i, u + 1, 0:8] = even[i]
                ring[0, i, u + 1, 8:16] = odd[i]
                ring[1, i, u, 8:16] = even[i]
                ring[1, i, u + 1, 0:8] = odd[i]
            return carry

        lax.fori_loop(0, 5, pairs, 0)
        windows = []
        for p in range(3):
            for q in range(3):
                f = 2 * half + p
                sides = []
                for d in range(2):
                    sides.append(
                        jnp.concatenate(
                            [
                                act[q, d, f : f + 2].reshape(-1, L),
                                act[q, 8 + d, f : f + 2].reshape(-1, L),
                                ring[d, 3 * p + q, 1:6].reshape(-1, L),
                            ],
                            axis=0,
                        )
                    )
                windows.append(jnp.concatenate(sides, axis=1))
        total = conv_rows(windows, near1, far1)
        acc[0, 2 * half : 2 * half + 2] = total[0:32].reshape(2, 16, L)
        acc[8, 2 * half : 2 * half + 2] = total[32:64].reshape(2, 16, L)
        racc[...] = total[64:].reshape(10, 8, L)
        lax.fori_loop(0, 9, functools.partial(finish, half), 0)

    def finish(half, m, carry):
        rim_rows = racc[m]
        left_half = lanes((8, L)) < C

        def by_pair(left, middle, right):
            return jnp.where(m == 0, left, middle), jnp.where(m == 8, right, middle)

        t0, t1 = by_pair(near[0], near[1], near[2])
        u0, u1 = by_pair(near[5], near[6], near[7])
        o0, o1 = by_pair(near[3], own_valid, near[4])
        limit = jnp.where(r8 < 2, jnp.where(left_half, t0, t1), jnp.where(left_half, u0, u1))
        outer = norm_silu(rim_rows + bias1, gain2)
        outer = jnp.where(first_frame + 2 * half + lax.rem(r8, 2) < limit, outer, 0.0)
        if half == 1:
            hring[m] = outer.astype(BF)
        limit = jnp.where(lanes((16, L)) < C, o0, o1)
        r16 = rows((16, L))
        for g in range(2):
            f = 2 * half + g
            v = acc[m, f]
            v = v + jnp.where(r16 == 0, rim_rows[4 + g : 5 + g], 0.0)
            v = v + jnp.where(r16 == 15, rim_rows[6 + g : 7 + g], 0.0)
            h = norm_silu(v + bias1, gain2)
            h = jnp.where(first_frame + f < limit, h, 0.0)
            hid[1, m, f + 2] = h.astype(BF)
            hid[0, m, f + 2] = down(h, outer[g : g + 1]).astype(BF)
            hid[2, m, f + 2] = up(h, outer[2 + g : 3 + g]).astype(BF)
        return carry

    rim(1)
    t_hid = [to_next(5, hid.at[1, :, 4:6], phid), to_next(6, hring, phring)]

    @pl.when(sends)
    def _():
        for copy in t_hid:
            copy.start()

    @pl.when(later)
    def _():
        t_snd.wait_recv()
        for copy in t_got:
            copy.wait_recv()

    side_pairs(pgot, (24, 20), 0, 2, pinner, keep)
    for m in range(8):
        pinner[m + 1] = keep(jnp.where(upper, wide(psnd, m), wide(psnd, 8 + m)))
    rim(0)

    def conv2(half):
        windows = []
        for p in range(3):
            for q in range(3):
                f = 2 * half + p
                windows.append(
                    jnp.concatenate(
                        [hid[q, 0:8, f : f + 2].reshape(-1, L), hid[q, 1:9, f : f + 2].reshape(-1, L)],
                        axis=1,
                    )
                )
        total = conv_rows(windows, near2, far2)
        total = total.reshape(8, 2, 16, L)
        for g in range(2):
            f = 2 * half + g
            there = first_frame + f < own_valid
            for m in range(8):
                x = vid[f, :, L * m : L * m + L].astype(F32)
                o = jnp.where(there, total[m, g] + bias2 + x, 0.0)
                out[f, 0, :, L * m : L * m + L] = o.astype(BF)

    conv2(1)

    @pl.when(later)
    def _():
        for copy in t_hid:
            copy.wait_recv()

    def before_2(m, carry):
        rim_rows = keep(phring[m].astype(F32))
        for f in range(2):
            h = keep(phid[m, f].astype(F32))
            hid[1, m, f] = h.astype(BF)
            hid[0, m, f] = down(h, rim_rows[f : f + 1]).astype(BF)
            hid[2, m, f] = up(h, rim_rows[2 + f : 3 + f]).astype(BF)
        return carry

    lax.fori_loop(0, 9, before_2, 0)
    conv2(0)

    def sent(k, carry):
        send_1(k).wait_send()
        send_2(k).wait_send()
        return carry

    lax.fori_loop(1, NT, sent, 0)

    @pl.when(is_corner)
    def _():
        def sent_c(k, carry):
            send_c(k).wait_send()
            return carry

        lax.fori_loop(1, NT, sent_c, 0)

    @pl.when(sends)
    def _():
        for copy in [t_act, t_snd, *t_got, *t_hid]:
            copy.wait_send()


def on_device(video, nbr, vf, g1, w1, b1, g2, w2, b2):
    vmem = lambda *shape, dtype=BF: pltpu.VMEM(shape, dtype)
    dma = lambda n: pltpu.SemaphoreType.DMA((n,))
    hbm = pl.BlockSpec(memory_space=pltpu.HBM)
    local = pl.BlockSpec(memory_space=pltpu.VMEM)
    return pl.pallas_call(
        kernel,
        out_shape=pltpu.VMEM(video.shape, BF),
        in_specs=[hbm] * 9,
        out_specs=local,
        scratch_shapes=[
            pltpu.SMEM((8, NT), jnp.int32),
            pltpu.SMEM((NT,), jnp.int32),
            *[vmem(C, dtype=F32)] * 4,
            vmem(4, 16, 16 * C),
            vmem(9, C, 3 * C),
            vmem(9, C, 3 * C),
            *[vmem(9, 256, C + L + 64)] * 4,
            vmem(3, 10, 6, 16, L),
            vmem(16, 8, L, dtype=F32),
            vmem(32, 8, L),
            vmem(NT + 1, 8, L),
            vmem(2, NT, 8, L),
            vmem(36, 8, L),
            vmem(8, 2, 16, L),
            vmem(16, 8, L),
            vmem(28, 8, L),
            vmem(10, 8, L, dtype=F32),
            vmem(10, 8, L, dtype=F32),
            vmem(2, 9, 6, 16, L),
            vmem(9, 4, 16, L, dtype=F32),
            vmem(10, 8, L, dtype=F32),
            vmem(3, 9, 6, 16, L),
            vmem(9, 8, L),
            vmem(9, 2, 16, L),
            vmem(9, 8, L),
            dma(9), dma(NT), dma(NT), dma(NT), dma(NT), dma(NT), dma(20), dma(7), dma(7),
        ],
        compiler_params=pltpu.CompilerParams(
            collective_id=0, has_side_effects=True, vmem_limit_bytes=66000000
        ),
    )(video, nbr.T, vf, g1, jnp.swapaxes(w1, 1, 2), b1, g2, jnp.swapaxes(w2, 1, 2), b2)


def solution(mesh):
    placed = (P("tm", "space", None, None), P(), P(), P(), P(), P(), P(), P(), P())
    return jax.shard_map(
        on_device, mesh=mesh, in_specs=placed, out_specs=P("tm", "space", None, None), check_vma=False
    )
```

time: 43.1 us -> 39 us (0.905)
  the two profiles are of different devices: /device:TPU:8 before, /device:TPU:2 now
where the time goes in v3:
time: 39 us; the launch traced here: 38.9 us
  Pallas kernels  38.1 us (98%)
  local copies, waits for them, and re-layouts  0.75 us (2%)
    pallas_call x1, Pallas kernels, on_device(): pl.pallas_call(kernel, out_shape=pltpu.VMEM(video.shape, BF), in_specs=[h...  38.1 us

profile of v3, /device:TPU:2, one launch (start us, length us, event | category | flops | bytes accessed | tf_op | source)
XLA Modules:
  0.0 38.9 jit_solution(10939458147270607319)
XLA Ops:
  0.0 38.1 %shard_map.91 = bf16[4,1,16,3072]{3,2,1,0:T(8,128)(2,1)S(1)} custom-call(bf16[4,1,16,3072]{3,2,1,0:T(8,128)(2,1)} %video.1, s32[8,32]{1,0:T(8,128)} %bitcast.5, s32[32]{0:T(128)} %vf_in.1, f32[192]{0:T(256)} %g1_in.1, bf16[9,192,576]{2,1,0:T(8,128)(2,1)} %bitcast.3, f32[192]{0:T(256)} %b1_in.1, f32[192]{0:T(256)} %g2_in.1, bf16[9,192,576]{2,1,0:T(8,128)(2,1)} %bitcast.4, ...), custom_call_target="tpu_custom_call" | custom-call | tf_op jit(solution)/shard_map/pallas_call | solution.py:523
  38.1 0.7 %copy.11 = bf16[4,1,16,3072]{3,2,1,0:T(8,128)(2,1)} copy(bf16[4,1,16,3072]{3,2,1,0:T(8,128)(2,1)S(1)} %shard_map.91) | data formatting | bytes 786432

commit v4 on v3

--- a/solution.py
+++ b/solution.py
@@ -54,14 +54,14 @@
 
 
 def matmul(a, b):
-    return lax.dot_general(a, b, (((1,), (1,)), ((), ())), preferred_element_type=F32)
+    return jnp.dot(a, b, preferred_element_type=F32)
 
 
 def conv_rows(windows, near_w, far_w):
     first = jnp.concatenate([w[:, : C + L + 64] for w in windows], axis=1)
     second = jnp.concatenate([w[:, 128:] for w in windows], axis=1)
-    near_w = jnp.concatenate([near_w[i] for i in range(9)], axis=1)
-    far_w = jnp.concatenate([far_w[i] for i in range(9)], axis=1)
+    near_w = near_w[...].reshape(-1, 256)
+    far_w = far_w[...].reshape(-1, 256)
     a, b = matmul(first, near_w), matmul(second, far_w)
     return jnp.concatenate([a[:, :128], a[:, 128:] + b[:, :128], b[:, 128:]], axis=1)
 
@@ -156,6 +156,14 @@
         snd[c] = strip32[c].astype(BF)
     got1[NT] = jnp.zeros((8, L), BF)
 
+    def widen(i, raw, near_w, far_w):
+        one, pad = raw[i], jnp.zeros((64, 3 * C), BF)
+        near_w[i, 0 : 3 * C] = jnp.concatenate([one, pad], axis=0).T
+        near_w[i, 3 * C : 3 * C + 64] = jnp.zeros((64, 256), BF)
+        far_w[i, 0:64] = jnp.zeros((64, 256), BF)
+        far_w[i, 64 : 64 + 3 * C] = jnp.concatenate([pad, one], axis=0).T
+
+
     pl.semaphore_wait(barrier, NT - 1 + jnp.where(later, 1, 0) + jnp.where(sends, 1, 0))
 
     def send_1(k):
@@ -182,13 +190,6 @@
         t_act.start()
         t_snd.start()
 
-    def widen(i, raw, near_w, far_w):
-        one, pad = raw[i], jnp.zeros((C, 64), BF)
-        near_w[i, 0:C] = jnp.concatenate([one, pad], axis=1)
-        near_w[i, C:256] = jnp.zeros((64, C + L + 64), BF)
-        far_w[i, 0:64] = jnp.zeros((64, C + L + 64), BF)
-        far_w[i, 64:256] = jnp.concatenate([pad, one], axis=1)
-
     load_1.wait()
 
     def widen_1(i, carry):
@@ -196,6 +197,13 @@
         return carry
 
     lax.fori_loop(0, 9, widen_1, 0)
+    load_2.wait()
+
+    def widen_2(i, carry):
+        widen(i, wr2, near2, far2)
+        return carry
+
+    lax.fori_loop(0, 9, widen_2, 0)
 
     def recv_1(k, carry):
         i = lax.rem(s + NT - k, NT)
@@ -274,14 +282,6 @@
                 )
             )
     acc[1:8] = conv_rows(windows, near1, far1).reshape(7, 4, 16, L)
-
-    load_2.wait()
-
-    def widen_2(i, carry):
-        widen(i, wr2, near2, far2)
-        return carry
-
-    lax.fori_loop(0, 9, widen_2, 0)
 
     def recv_2(k, carry):
         i = lax.rem(s + NT - k, NT)
@@ -532,7 +532,7 @@
             vmem(4, 16, 16 * C),
             vmem(9, C, 3 * C),
             vmem(9, C, 3 * C),
-            *[vmem(9, 256, C + L + 64)] * 4,
+            *[vmem(9, C + L + 64, 256)] * 4,
             vmem(3, 10, 6, 16, L),
             vmem(16, 8, L, dtype=F32),
             vmem(32, 8, L),

time: 39 us -> 36.9 us (0.946)
  Pallas kernels: 38.1 us -> 36 us
    pallas_call x1, Pallas kernels: 38.1 us -> 36 us  [on_device(): pl.pallas_call(kernel, out_shape=pltpu.VMEM(video.shape, BF), in_specs=[h...]
where the time goes in v4:
time: 36.9 us; the launch traced here: 36.8 us
  Pallas kernels  36 us (98%)
  local copies, waits for them, and re-layouts  0.75 us (2%)
    pallas_call x1, Pallas kernels, on_device(): pl.pallas_call(kernel, out_shape=pltpu.VMEM(video.shape, BF), in_specs=[h...  36 us
    unnamed x1, local copies, waits for them, and re-layouts  0.75 us

profile of v4, /device:TPU:2, one launch (start us, length us, event | category | flops | bytes accessed | tf_op | source)
XLA Modules:
  0.0 36.8 jit_solution(1513221619044548272)
XLA Ops:
  0.0 36.0 %shard_map.91 = bf16[4,1,16,3072]{3,2,1,0:T(8,128)(2,1)S(1)} custom-call(bf16[4,1,16,3072]{3,2,1,0:T(8,128)(2,1)} %video.1, s32[8,32]{1,0:T(8,128)} %bitcast.5, s32[32]{0:T(128)} %vf_in.1, f32[192]{0:T(256)} %g1_in.1, bf16[9,192,576]{2,1,0:T(8,128)(2,1)} %bitcast.3, f32[192]{0:T(256)} %b1_in.1, f32[192]{0:T(256)} %g2_in.1, bf16[9,192,576]{2,1,0:T(8,128)(2,1)} %bitcast.4, ...), custom_call_target="tpu_custom_call" | custom-call | tf_op jit(solution)/shard_map/pallas_call | solution.py:523
  36.0 0.7 %copy.11 = bf16[4,1,16,3072]{3,2,1,0:T(8,128)(2,1)} copy(bf16[4,1,16,3072]{3,2,1,0:T(8,128)(2,1)S(1)} %shard_map.91) | data formatting | bytes 786432

commit v5 on v4

--- a/solution.py
+++ b/solution.py
@@ -17,14 +17,18 @@
 
 
 def chunk_of(dev):
+    odd = lax.rem(lax.axis_index("tm"), 2)
     z, y = lax.div(dev, 4), lax.rem(dev, 4)
+    y = y + odd * (1 - 2 * lax.rem(y, 2))
     strip = lax.rem(y, 2) * 2 + lax.div(y, 2)
     return strip * 8 + lax.rem(3 * (z + 16 - 2 * strip), 8)
 
 
 def device_of(chunk):
+    odd = lax.rem(lax.axis_index("tm"), 2)
     strip, low = chunk // 8, chunk % 8
-    return ((3 * low + 2 * strip) % 8) * 4 + (strip % 2) * 2 + strip // 2
+    y = (strip % 2) * 2 + strip // 2
+    return ((3 * low + 2 * strip) % 8) * 4 + y + odd * (1 - 2 * (y % 2))
 
 
 def offset(i):
@@ -92,7 +96,7 @@
         pl.semaphore_signal(barrier, inc=1, device_id={"space": lax.rem(s + offset(i), NT)})
         return carry
 
-    lax.fori_loop(0, NT - 1, greet, 0)
+    lax.fori_loop(0, NT - 1, greet, 0, unroll=True)
 
     @pl.when(sends)
     def _():
@@ -227,7 +231,7 @@
         snd2[1, d] = got1[nbr[cside, d]]
         return carry
 
-    lax.fori_loop(0, NT, pick, 0)
+    lax.fori_loop(0, NT, pick, 0, unroll=True)
 
     def send_2(k):
         d = lax.rem(s + k, NT)
@@ -282,6 +286,17 @@
                 )
             )
     acc[1:8] = conv_rows(windows, near1, far1).reshape(7, 4, 16, L)
+
+    def early(m, carry):
+        for f in range(4):
+            h = norm_silu(acc[m, f] + bias1, gain2)
+            h = jnp.where(first_frame + f < own_valid, h, 0.0)
+            hid[1, m, f + 2] = h.astype(BF)
+            hid[0, m, f + 2] = down(h, zero_row).astype(BF)
+            hid[2, m, f + 2] = up(h, zero_row).astype(BF)
+        return carry
+
+    lax.fori_loop(1, 8, early, 0)
 
     def recv_2(k, carry):
         i = lax.rem(s + NT - k, NT)
@@ -404,7 +419,9 @@
         acc[0, 2 * half : 2 * half + 2] = total[0:32].reshape(2, 16, L)
         acc[8, 2 * half : 2 * half + 2] = total[32:64].reshape(2, 16, L)
         racc[...] = total[64:].reshape(10, 8, L)
-        lax.fori_loop(0, 9, functools.partial(finish, half), 0)
+        finish(half, 0, 0)
+        finish(half, 8, 0)
+        lax.fori_loop(1, 8, functools.partial(finish_rows, half), 0)
 
     def finish(half, m, carry):
         rim_rows = racc[m]
@@ -433,6 +450,29 @@
             hid[1, m, f + 2] = h.astype(BF)
             hid[0, m, f + 2] = down(h, outer[g : g + 1]).astype(BF)
             hid[2, m, f + 2] = up(h, outer[2 + g : 3 + g]).astype(BF)
+        return carry
+
+    def finish_rows(half, m, carry):
+        edge = racc[m]
+        for g in range(2):
+            v = acc[m, 2 * half + g]
+            edge = edge + jnp.where(r8 == 4 + g, v[0:1], 0.0) + jnp.where(r8 == 6 + g, v[15:16], 0.0)
+        limit = jnp.where(r8 < 2, near[1], jnp.where(r8 < 4, near[6], own_valid))
+        edge = norm_silu(edge + bias1, gain2)
+        edge = jnp.where(first_frame + 2 * half + lax.rem(r8, 2) < limit, edge, 0.0)
+        if half == 1:
+            hring[m] = edge.astype(BF)
+        r16 = rows((16, L))
+        for g in range(2):
+            f = 2 * half + g + 2
+            above, below = edge[g : g + 1], edge[2 + g : 3 + g]
+            first, last = edge[4 + g : 5 + g], edge[6 + g : 7 + g]
+            h = hid[1, m, f].astype(F32)
+            hid[1, m, f] = jnp.where(r16 == 0, first, jnp.where(r16 == 15, last, h)).astype(BF)
+            h = hid[0, m, f].astype(F32)
+            hid[0, m, f] = jnp.where(r16 == 0, above, jnp.where(r16 == 1, first, h)).astype(BF)
+            h = hid[2, m, f].astype(F32)
+            hid[2, m, f] = jnp.where(r16 == 15, below, jnp.where(r16 == 14, last, h)).astype(BF)
         return carry
 
     rim(1)

time: 36.9 us -> 36.2 us (0.981)
  Pallas kernels: 36 us -> 35.4 us
    pallas_call x1, Pallas kernels: 36 us -> 35.4 us  [on_device(): pl.pallas_call(kernel, out_shape=pltpu.VMEM(video.shape, BF), in_specs=[h...]
where the time goes in v5:
time: 36.2 us; the launch traced here: 36.1 us
  Pallas kernels  35.4 us (98%)
  local copies, waits for them, and re-layouts  0.75 us (2%)
    pallas_call x1, Pallas kernels, on_device(): pl.pallas_call(kernel, out_shape=pltpu.VMEM(video.shape, BF), in_specs=[h...  35.4 us
    unnamed x1, local copies, waits for them, and re-layouts  0.75 us

profile of v5, /device:TPU:2, one launch (start us, length us, event | category | flops | bytes accessed | tf_op | source)
XLA Modules:
  0.0 36.1 jit_solution(12079349124872779607)
XLA Ops:
  0.0 35.4 %shard_map.91 = bf16[4,1,16,3072]{3,2,1,0:T(8,128)(2,1)S(1)} custom-call(bf16[4,1,16,3072]{3,2,1,0:T(8,128)(2,1)} %video.1, s32[8,32]{1,0:T(8,128)} %bitcast.5, s32[32]{0:T(128)} %vf_in.1, f32[192]{0:T(256)} %g1_in.1, bf16[9,192,576]{2,1,0:T(8,128)(2,1)} %bitcast.3, f32[192]{0:T(256)} %b1_in.1, f32[192]{0:T(256)} %g2_in.1, bf16[9,192,576]{2,1,0:T(8,128)(2,1)} %bitcast.4, ...), custom_call_target="tpu_custom_call" | custom-call | tf_op jit(solution)/shard_map/pallas_call | solution.py:563
  35.4 0.7 %copy.11 = bf16[4,1,16,3072]{3,2,1,0:T(8,128)(2,1)} copy(bf16[4,1,16,3072]{3,2,1,0:T(8,128)(2,1)S(1)} %shard_map.91) | data formatting | bytes 786432
